TPU v7x, 32 devices: a whole 2x2x4 slice. The times are simulated.
32 devices in a mesh: gx: 8 (over z, x), gy: 4 (over y, core).
Axes of the slice: x: 2, y: 2, z: 4, core: 2. Of those that a mesh axis runs over, the one named last changes fastest.
Arguments:
- pooled: bfloat16 [4096, 8, 128], P(('gx', 'gy')), may hold values from -6 to 6
- cotangent: bfloat16 [4096, 28, 128], P(('gx', 'gy')), may hold values from -0.09375 to 0.09375
- bilinear: bfloat16 [7, 128, 128], replicated, may hold values from -0.5 to 0.5
- bag_ids: int32 [4096, 8, 4], P(('gx', 'gy')), may hold values from 0 to 8191, as said below
- bag_lens: int32 [4096, 8], P(('gx', 'gy')), may hold values from 1 to 4
- row_home: int32 [8, 8192], replicated, may hold values from 0 to 8191, as said below
Outputs:
- weight_grad: float32 [7, 128, 128], replicated
- table_grad: float32 [8192, 8, 128], P(('gx', 'gy'))
Inputs may be any that keep to these rules, and one draw needn't show every extreme that they name: Each row row_home[f] is a permutation; row r of field f's table is stored at position row_home[f, r] of table_grad's first dimension. Only the first bag_lens entries of a bag are live. The stored position q = row_home[f, bag_ids[sample, f, k]] of an entry lies in the block of 256 positions of device q // 256 (devices in gx+gy order); among all entries of one device's samples, live or not, at most 256 lie in any one device's block; in every device's entries some block is hit exactly 256 times, and one block is hit exactly 256 times by the entries of every device.
All inputs are finite; a program needn't handle non-finite values.
Results may differ from a plain program's by a relative error of at most 0.0035.
Values may be sent and summed in bfloat16 or wider, within the bound.
A program may use at most 64 MiB of HBM per device.

v0:
```python
import functools

import jax
import jax.numpy as jnp
from jax import lax
from jax.experimental import pallas as pl
from jax.experimental.pallas import tpu as pltpu
from jax.sharding import PartitionSpec as P

MESH = pl.DeviceIdType.MESH
BF = jnp.bfloat16
F32 = jnp.float32
LANES = 128


def pair_list(fields):
    return [(i, j) for i in range(fields) for j in range(i + 1, fields)]


def kernel(
    size_gx, size_gy,
    pooled_ref, cot_ref, bil_ref, bag_ref, lens_ref, home_ref,
    out_ref, wout_ref,
    pool_f, proj_f, meta,
    gath, part, got,
    w0, w1, w2, w2s, w3, w3s,
    zs, zr, ss, sr, ps, pr,
    w1s_sem, w1r_sem, w2s_sem, w2r_sem, w3s_sem, w3r_sem,
):
    samples, fields, width = pooled_ref.shape
    bag = bag_ref.shape[1]
    rows = part.shape[2]
    piece = w0.shape[1]
    nz, ny = size_gx // 2, size_gy // 2
    plane = 2 * size_gy
    npc = 2 * ny
    gx, gy = lax.axis_index("gx"), lax.axis_index("gy")
    z, x, y, c = gx // 2, gx % 2, gy // 2, gy % 2
    spot = x * ny + y
    seat = x * size_gy + gy
    sibling = (gx, y * 2 + 1 - c)

    def spot_peer(d):
        to = (spot + d) % npc
        return (z * 2 + to // ny, (to % ny) * 2 + c)

    def z_peer(d):
        return (((z + d) % nz) * 2 + x, gy)

    def seat_peer(d):
        to = (seat + d) % plane
        return (z * 2 + to // size_gy, to % size_gy)

    def remote(src, dst, send, recv, dev):
        return pltpu.make_async_remote_copy(
            src_ref=src, dst_ref=dst, send_sem=send, recv_sem=recv,
            device_id=dev, device_id_type=MESH,
        )

    def z_copy(f, d):
        i = f * nz + d
        return remote(gath.at[f, 0, 0], gath.at[f, 0, d], zs.at[i], zr.at[i], z_peer(d))

    def s_copy(f, d):
        i = f * nz + d
        return remote(gath.at[f, 0, d], gath.at[f, 1, d], ss.at[i], sr.at[i], sibling)

    def p_copy(f, d):
        i = f * npc + d
        return remote(part.at[d, f], got.at[d, f], ps.at[i], pr.at[i], spot_peer(d))

    def w1_copy(d):
        return remote(
            w0.at[(seat + d) % plane], w1.at[d], w1s_sem.at[d], w1r_sem.at[d], seat_peer(d)
        )

    def w2_copy(d, slot):
        return remote(w2s, w2.at[slot], w2s_sem.at[d], w2r_sem.at[slot], z_peer(d))

    def w3_copy(d, slot):
        return remote(w3s, w3.at[slot], w3s_sem.at[d], w3r_sem.at[slot], seat_peer(d))

    barrier = pltpu.get_barrier_semaphore()
    for d in range(1, nz):
        pl.semaphore_signal(barrier, inc=1, device_id=z_peer(d), device_id_type=MESH)
    for d in range(1, plane):
        pl.semaphore_signal(barrier, inc=1, device_id=seat_peer(d), device_id_type=MESH)

    def spread_out(b, carry):
        pool_f[pl.ds(pl.multiple_of(b * fields, fields), fields), :] = pooled_ref[b].astype(F32)
        return carry

    lax.fori_loop(0, samples, spread_out, 0, unroll=8)

    bags = [bag_ref[:, k, :] for k in range(bag)]
    high = [b // LANES for b in bags]
    low = [b % LANES for b in bags]

    def look(h, found):
        row = home_ref[:, pl.ds(pl.multiple_of(h * LANES, LANES), LANES)]
        return tuple(
            jnp.where(high[k] == h, jnp.take_along_axis(row, low[k], axis=1), found[k])
            for k in range(bag)
        )

    none = jnp.full(lens_ref.shape, 0, jnp.int32)
    found = lax.fori_loop(0, home_ref.shape[1] // LANES, look, (none,) * bag, unroll=8)
    lens = lens_ref[...]
    for k in range(bag):
        meta[:, k, :] = jnp.where(lens > k, found[k] // rows, -1).astype(F32)
        meta[:, bag + k, :] = (found[k] % rows).astype(F32)

    pool = lambda f: pool_f[pl.ds(f, samples, stride=fields), :]
    number = {pair: p for p, pair in enumerate(pair_list(fields))}
    cot = lambda i, j: cot_ref[number[i, j]].astype(F32)

    for i in range(fields):
        total = None
        if i < fields - 1:
            mine = pool(i).astype(BF)
            proj_f[i] = jnp.dot(mine, bil_ref[i], preferred_element_type=F32)
            upper = jnp.zeros((samples, width), F32)
            for j in range(i + 1, fields):
                upper = upper + cot(i, j) * pool(j)
            upper = upper.astype(BF)
            wide_w = lax.dot_general(
                mine, upper, (((0,), (0,)), ((), ())), preferred_element_type=F32
            ).astype(BF)
            at, end = i * width, (i + 1) * width
            while at < end:
                p, r = at // piece, at % piece
                n = min(piece - r, end - at)
                w0[p, r : r + n, :] = wide_w[at - i * width : at - i * width + n, :]
                at += n
            total = lax.dot_general(
                upper, bil_ref[i], (((1,), (1,)), ((), ())), preferred_element_type=F32
            )
        for k in range(i):
            term = cot(k, i) * proj_f[k]
            total = term if total is None else total + term
        gath[i, 0, 0, :samples, :] = total.astype(BF)
        gath[i, 0, 0, samples:, :] = meta[i].astype(BF)
        if i == 0:
            pl.semaphore_wait(barrier, nz - 1 + plane - 1)

        for d in range(1, nz):
            z_copy(i, d).start()
        s_copy(i, 0).start()

    for d in range(1, plane):
        w1_copy(d).start()

    def forward(f):
        for d in range(1, nz):
            z_copy(f, d).wait_recv()
            s_copy(f, d).start()

    row_number = lax.broadcasted_iota(jnp.int32, (rows, samples), 0).astype(F32).astype(BF)
    one, zero = jnp.ones((), BF), jnp.zeros((), BF)

    def sums_for(f, d):
        gx_to, gy_to = spot_peer(d)
        owner = (gx_to * size_gy + gy_to).astype(F32)
        blocks, values = [], []
        for core in range(2):
            for s in range(nz):
                note = gath[f, core, s, samples:, :].astype(F32)
                key = jnp.where(note[:bag] == owner, note[bag:], -1.0).astype(BF)
                count = None
                for k in range(bag):
                    hit = jnp.where(row_number == key[k : k + 1, :], one, zero)
                    count = hit if count is None else count + hit
                blocks.append(count)
                values.append(gath[f, core, s, :samples, :])
        return jnp.dot(
            jnp.concatenate(blocks, axis=1),
            jnp.concatenate(values, axis=0),
            preferred_element_type=F32,
        )

    def weights_in_plane():
        total = w0[seat].astype(F32)
        for d in range(1, plane):
            w1_copy(d).wait_recv()
            total = total + w1[d].astype(F32)
        w2s[...] = total
        w2[z] = total
        for d in range(1, nz):
            w2_copy(d, z).start()

    def weights_along_z():
        for d in range(1, nz):
            w2_copy(d, (z + d) % nz).wait_recv()
        total = w2[0]
        for s in range(1, nz):
            total = total + w2[s]
        w3s[...] = total.astype(BF)
        w3[seat] = total.astype(BF)
        for d in range(1, plane):
            w3_copy(d, seat).start()

    forward(0)

    def one_field(f, carry):
        @pl.when(f + 1 < fields)
        def _():
            forward(f + 1)

        for d in range(nz):
            s_copy(f, d).wait_recv()

        def one_target(d, inner):
            part[d, f] = sums_for(f, d).astype(BF)
            p_copy(f, d).start()
            return inner

        lax.fori_loop(1, npc, one_target, 0)
        out_ref[pl.ds(f, rows, stride=fields), :] = sums_for(f, 0)

        @pl.when(f == 1)
        def _():
            weights_in_plane()

        @pl.when(f == 3)
        def _():
            weights_along_z()

        return carry

    lax.fori_loop(0, fields, one_field, 0)

    for d in range(1, plane):
        w3_copy(d, (seat + d) % plane).wait_recv()
    wout_ref[...] = w3[...].astype(F32)

    def finish(f, carry):
        at = pl.ds(f, rows, stride=fields)
        total = out_ref[at, :]
        for d in range(1, npc):
            p_copy(f, d).wait_recv()
            total = total + got[d, f].astype(F32)
        out_ref[at, :] = total
        return carry

    lax.fori_loop(0, fields, finish, 0)

    def drain(f, carry):
        for d in range(1, nz):
            z_copy(f, d).wait_send()
        for d in range(nz):
            s_copy(f, d).wait_send()
        for d in range(1, npc):
            p_copy(f, d).wait_send()
        return carry

    lax.fori_loop(0, fields, drain, 0)
    for d in range(1, nz):
        w2_copy(d, z).wait_send()
    for d in range(1, plane):
        w1_copy(d).wait_send()
        w3_copy(d, seat).wait_send()


def on_device(size_gx, size_gy, pooled, cotangent, bilinear, bag_ids, bag_lens, row_home):
    samples, fields, width = pooled.shape
    bag = bag_ids.shape[2]
    rows = row_home.shape[1] // (size_gx * size_gy)
    nz, ny, plane = size_gx // 2, size_gy // 2, 2 * size_gy
    npc = 2 * ny
    piece = (fields - 1) * width // plane
    vmem = pl.BlockSpec(memory_space=pltpu.VMEM)
    dma = pltpu.SemaphoreType.DMA
    table, weight = pl.pallas_call(
        functools.partial(kernel, size_gx, size_gy),
        out_shape=(
            jax.ShapeDtypeStruct((rows * fields, width), F32),
            jax.ShapeDtypeStruct((plane, piece, width), F32),
        ),
        in_specs=[vmem] * 6,
        out_specs=(vmem,) * 2,
        scratch_shapes=[
            pltpu.VMEM((samples * fields, width), F32),
            pltpu.VMEM((fields - 1, samples, width), F32),
            pltpu.VMEM((fields, 2 * bag, samples), F32),
            pltpu.VMEM((fields, 2, nz, samples + 2 * bag, width), BF),
            pltpu.VMEM((npc, fields, rows, width), BF),
            pltpu.VMEM((npc, fields, rows, width), BF),
            pltpu.VMEM((plane, piece, width), BF),
            pltpu.VMEM((plane, piece, width), BF),
            pltpu.VMEM((nz, piece, width), F32),
            pltpu.VMEM((piece, width), F32),
            pltpu.VMEM((plane, piece, width), BF),
            pltpu.VMEM((piece, width), BF),
            dma((fields * nz,)),
            dma((fields * nz,)),
            dma((fields * nz,)),
            dma((fields * nz,)),
            dma((fields * npc,)),
            dma((fields * npc,)),
            dma((plane,)),
            dma((plane,)),
            dma((nz,)),
            dma((nz,)),
            dma((plane,)),
            dma((plane,)),
        ],
        compiler_params=pltpu.CompilerParams(collective_id=0, has_side_effects=True),
    )(
        pooled, cotangent.transpose(1, 0, 2), bilinear,
        bag_ids.transpose(1, 2, 0), bag_lens.transpose(1, 0), row_home,
    )
    return (
        weight.reshape(fields - 1, width, width),
        table.reshape(rows, fields, width),
    )


def solution(mesh):
    placed = (
        P(("gx", "gy"), None, None),
        P(("gx", "gy"), None, None),
        P(),
        P(("gx", "gy"), None, None),
        P(("gx", "gy"), None),
        P(),
    )
    return jax.shard_map(
        functools.partial(on_device, mesh.shape["gx"], mesh.shape["gy"]),
        mesh=mesh,
        in_specs=placed,
        out_specs=(P(), P(("gx", "gy"), None, None)),
        check_vma=False,
    )
```

profile of v0, /device:TPU:0, one launch (start us, length us, event | category | flops | bytes accessed | tf_op | source)
XLA Modules:
  0.0 59.1 jit_solution(9261402214941111325)
XLA Ops:
  0.6 54.4 %shard_map.77 = (f32[2048,128]{1,0:T(8,128)}, f32[8,112,128]{2,1,0:T(8,128)}) custom-call(bf16[128,8,128]{2,1,0:T(8,128)(2,1)} %pooled_ref.1, bf16[28,128,128]{2,1,0:T(8,128)(2,1)} %bitcast.6, bf16[7,128,128]{2,1,0:T(8,128)(2,1)} %bil_ref.1, s32[8,4,128]{2,1,0:T(4,128)} %bitcast.8, s32[8,128]{1,0:T(8,128)} %bitcast.9, s32[8,8192]{1,0:T(8,128)} %home_ref.1), custom_call_target="tpu_custom_call" | custom-call | tf_op jit(solution)/shard_map/pallas_call | solution.py:273
  55.1 1.8 %copy.10 = f32[7,128,128]{2,1,0:T(8,128)} copy(f32[7,128,128]{2,1,0:T(8,128)} %bitcast.7) | data formatting | bytes 917504
  56.9 2.3 %copy.11 = f32[256,8,128]{2,1,0:T(8,128)} copy(f32[256,8,128]{2,1,0:T(8,128)} %bitcast.5) | data formatting | bytes 2097152
where the time goes:
time: 59.4 us; the launch traced here: 59.1 us
  Pallas kernels  54.4 us (92%)
  local copies, waits for them, and re-layouts  4.08 us (7%)
  between operations  0.64 us (1%)
    pallas_call x1, Pallas kernels, on_device(): pl.pallas_call(functools.partial(kernel, size_gx, size_gy), out_shape=(ja...  54.4 us
    unnamed x2, local copies, waits for them, and re-layouts  4.08 us

commit v1 on v0

v1 whole, which is shorter than its diff:
```python
import functools
import math

import jax
import jax.numpy as jnp
from jax import lax
from jax.experimental import pallas as pl
from jax.experimental.pallas import tpu as pltpu
from jax.sharding import PartitionSpec as P

MESH = pl.DeviceIdType.MESH
BF = jnp.bfloat16
F32 = jnp.float32
LANES = 128
AHEAD = 1
DIRECT = 1
LAG_SECOND = 3
LAG_FINAL = 5


def pair_list(fields):
    return [(i, j) for i in range(fields) for j in range(i + 1, fields)]


def kernel(
    size_gx, size_gy,
    pooled_hbm, cot_hbm, bil_hbm, bag_hbm, lens_hbm, home_hbm,
    out_ref, wout_ref,
    pooled_ref, cot_ref, bil_ref, bag_ref, lens_ref, home_ref,
    pool_f, proj_f,
    notes, gath, keep, part1, got1, part2, got2,
    w0, wsib, w1s, w1, w2, w3,
    ls, cs,
    ms, mr, zs, zr, ss, sr, p1s, p1r, p2s, p2r,
    was, war, w1ss, w1rs, w2ss, w2rs, w3ss, w3rs, wbs, wbr,
):
    samples, fields, width = pooled_ref.shape
    bag = bag_ref.shape[1]
    rows = keep.shape[2]
    nz, ny = size_gx // 2, size_gy // 2
    npc = 2 * ny
    gx, gy = lax.axis_index("gx"), lax.axis_index("gy")
    z, x, y, c = gx // 2, gx % 2, gy // 2, gy % 2
    spot = x * ny + y
    sibling = (gx, y * 2 + 1 - c)
    across = (z * 2 + 1 - x, gy)

    def spot_peer(d):
        to = (spot + d) % npc
        return (z * 2 + to // ny, (to % ny) * 2 + c)

    def row_peer(d):
        return (gx, ((y + d) % ny) * 2 + c)

    def z_peer(d):
        return (((z + d) % nz) * 2 + x, gy)

    def z_side(up, hop=1):
        return ((z + hop if up else z - hop) * 2 + x, gy)

    def z_reaches(up, hop=1):
        return z < nz - hop if up else z >= hop

    def remote(src, dst, send, recv, dev):
        return pltpu.make_async_remote_copy(
            src_ref=src, dst_ref=dst, send_sem=send, recv_sem=recv,
            device_id=dev, device_id_type=MESH,
        )

    def m_copy(s, up, hop=1):
        return remote(
            notes.at[0, s], notes.at[0, s], ms.at[int(up) + 2 * (hop - 1), s], mr.at[0, s],
            z_side(up, hop),
        )

    def ms_copy(s):
        return remote(notes.at[0, s], notes.at[1, s], ms.at[4, s], mr.at[1, s], sibling)

    def z_copy(f, s, up, hop=1):
        i = f * nz + s
        return remote(
            gath.at[f, 0, s], gath.at[f, 0, s], zs.at[int(up) + 2 * (hop - 1), i], zr.at[i],
            z_side(up, hop),
        )

    def s_copy(f, s):
        i = f * nz + s
        return remote(gath.at[f, 0, s], gath.at[f, 1, s], ss.at[i], sr.at[i], sibling)

    def first_copy(f, j, dev):
        return remote(part1.at[f, j], got1.at[f, j], p1s.at[f, j], p1r.at[f, j], dev)

    def second_copy(f, j, dev):
        return remote(part2.at[f, j], got2.at[f, j], p2s.at[f, j], p2r.at[f, j], dev)

    def wa_copy():
        return remote(w0.at[pl.ds((1 - c) * npc, npc)], wsib, was.at[0], war.at[0], sibling)

    def w1_copy(d):
        return remote(w1s.at[(spot + d) % npc], w1.at[d], w1ss.at[d], w1rs.at[d], spot_peer(d))

    def w2_copy(d, slot):
        return remote(w2.at[z], w2.at[slot], w2ss.at[d], w2rs.at[slot], z_peer(d))

    def w3_copy(d, slot):
        return remote(
            w3.at[c * npc + spot], w3.at[slot], w3ss.at[d], w3rs.at[d], spot_peer(d)
        )

    def wb_copy(half):
        at = pl.ds(half * npc, npc)
        return remote(w3.at[at], w3.at[at], wbs.at[0], wbr.at[0], sibling)

    pairs = pair_list(fields)
    number = {pair: p for p, pair in enumerate(pairs)}
    first = [number[i, i + 1] for i in range(fields - 1)]

    def cot_load(i):
        at = pl.ds(first[i], fields - 1 - i)
        return pltpu.make_async_copy(cot_hbm.at[at], cot_ref.at[at], cs.at[i])

    loads = [
        pltpu.make_async_copy(src, dst, ls.at[n])
        for n, (src, dst) in enumerate([
            (pooled_hbm, pooled_ref), (bil_hbm, bil_ref), (bag_hbm, bag_ref),
            (lens_hbm, lens_ref), (home_hbm, home_ref),
        ])
    ]
    loads[0].start()
    cot_load(0).start()
    for load in loads[1:]:
        load.start()
    for i in range(1, fields - 1):
        cot_load(i).start()

    barrier = pltpu.get_barrier_semaphore()
    for d in range(1, nz):
        pl.semaphore_signal(barrier, inc=1, device_id=z_peer(d), device_id_type=MESH)
    for d in range(1, npc):
        pl.semaphore_signal(barrier, inc=1, device_id=spot_peer(d), device_id_type=MESH)
    pl.semaphore_signal(barrier, inc=1, device_id=sibling, device_id_type=MESH)

    def spread_out(b, carry):
        pool_f[pl.ds(pl.multiple_of(b * fields, fields), fields), :] = pooled_ref[b].astype(F32)
        return carry

    def write_notes():
        for load in loads[2:]:
            load.wait()
        bags = [bag_ref[:, k, :] for k in range(bag)]
        high = [b // LANES for b in bags]
        low = [b % LANES for b in bags]

        def look(h, found):
            row = home_ref[:, pl.ds(pl.multiple_of(h * LANES, LANES), LANES)]
            return tuple(
                jnp.where(high[k] == h, jnp.take_along_axis(row, low[k], axis=1), found[k])
                for k in range(bag)
            )

        none = jnp.full(lens_ref.shape, 0, jnp.int32)
        found = lax.fori_loop(0, home_ref.shape[1] // LANES, look, (none,) * bag, unroll=8)
        lens = lens_ref[...]
        live = [jnp.where(lens > k, found[k], -1) for k in range(bag)]
        for k in range(bag):
            times = None
            for other in live:
                same = jnp.where(live[k] == other, 1, 0)
                times = same if times is None else times + same
            notes[0, z, :, k, :] = live[k] * 8 + jnp.where(live[k] < 0, 0, times)

    loads[0].wait()
    lax.fori_loop(0, samples, spread_out, 0, unroll=8)
    loads[1].wait()

    pool = lambda f: pool_f[pl.ds(f, samples, stride=fields), :]
    cot = lambda i, j: cot_ref[number[i, j]].astype(F32)
    piece = w0.shape[1]

    def send_own(copy):
        for hop in (2, 1):
            for up in (False, True):
                @pl.when(z_reaches(up, hop))
                def _():
                    copy(up, hop).start()

    for i in range(fields):
        total = None
        if i < fields - 1:
            cot_load(i).wait()
            mine = pool(i).astype(BF)
            upper = jnp.zeros((samples, width), F32)
            for j in range(i + 1, fields):
                upper = upper + cot(i, j) * pool(j)
            upper = upper.astype(BF)
            total = lax.dot_general(
                upper, bil_ref[i], (((1,), (1,)), ((), ())), preferred_element_type=F32
            )
        for k in range(i):
            term = cot(k, i) * proj_f[k]
            total = term if total is None else total + term
        gath[i, 0, z] = total.astype(BF)
        if i == 0:
            pl.semaphore_wait(barrier, nz - 1 + npc - 1 + 1)
        send_own(lambda up, hop: z_copy(i, z, up, hop))
        s_copy(i, z).start()
        if i == 0:
            write_notes()
            send_own(lambda up, hop: m_copy(z, up, hop))
            ms_copy(z).start()
        if i < fields - 1:
            proj_f[i] = jnp.dot(mine, bil_ref[i], preferred_element_type=F32)
            wide_w = lax.dot_general(
                mine, upper, (((0,), (0,)), ((), ())), preferred_element_type=F32
            )
            at, end = i * width, (i + 1) * width
            while at < end:
                p, r = at // piece, at % piece
                n = min(piece - r, end - at)
                w0[p, r : r + n, :] = wide_w[at - i * width : at - i * width + n, :]
                at += n

    wa_copy().start()

    def take(arrived, onward, to_sibling):
        for o in range(1, nz):
            for up in (True, False):
                s = z - o if up else z + o

                @pl.when(s >= 0 if up else s < nz)
                def _():
                    arrived(s)

                    if o > 1:
                        @pl.when(z_reaches(up))
                        def _():
                            onward(s, up)

                    to_sibling(s)

    def receive(f):
        take(
            lambda s: z_copy(f, s, True).wait_recv(),
            lambda s, up: z_copy(f, s, up).start(),
            lambda s: s_copy(f, s).start(),
        )

    take(
        lambda s: m_copy(s, True).wait_recv(),
        lambda s, up: m_copy(s, up).start(),
        lambda s: ms_copy(s).start(),
    )

    for s in range(nz):
        ms_copy(s).wait_recv()

    row_number = lax.broadcasted_iota(jnp.int32, (rows, samples), 0).astype(F32).astype(BF)
    zero = jnp.zeros((), BF)

    def sums_for(f, x_to, y_to):
        base = ((z * 2 + x_to) * size_gy + y_to * 2 + c) * rows
        blocks, values = [], []
        for core in range(2):
            for s in range(nz):
                note = notes[core, s, f]
                key = ((note >> 3) - base).astype(F32).astype(BF)
                times = (note & 7).astype(F32).astype(BF)
                count = zero
                for k in range(bag):
                    count = jnp.where(
                        row_number == key[k : k + 1, :], times[k : k + 1, :], count
                    )
                blocks.append(count)
                values.append(gath[f, core, s])
        return jnp.dot(
            jnp.concatenate(blocks, axis=1),
            jnp.concatenate(values, axis=0),
            preferred_element_type=F32,
        )

    def by_x(f):
        return jnp.logical_and(f % 2 == 0, f < fields - DIRECT)

    def by_y(f):
        return jnp.logical_and(f % 2 == 1, f < fields - DIRECT)

    def straight(f):
        return f >= fields - DIRECT

    def field_sums(f):
        for s in range(nz):
            s_copy(f, s).wait_recv()

        def one_target(j, carry):
            d_x = jnp.where(j < ny, j, j - ny + 1)
            d_y = jnp.where(j == npc - 2, 0, jnp.where(j < ny - 1, j + 1, j - ny + 2))
            other_x, other_y = j < ny, jnp.logical_or(j < ny - 1, j == npc - 2)
            d = jnp.where(by_x(f), d_x, d_y)
            x_to = jnp.where(jnp.where(by_x(f), other_x, other_y), 1 - x, x)
            y_to = (y + d) % ny
            to = (spot + npc - 1 - j) % npc
            x_to = jnp.where(straight(f), to // ny, x_to)
            y_to = jnp.where(straight(f), to % ny, y_to)
            mine = j == npc - 1
            total = sums_for(f, jnp.where(mine, x, x_to), jnp.where(mine, y, y_to))
            sent = jnp.where(by_x(f), j < ny, jnp.where(by_y(f), j < npc - 2, j < npc - 1))

            @pl.when(sent)
            def _():
                part1[f, j] = total.astype(BF)

                @pl.when(by_x(f))
                def _():
                    first_copy(f, j, across).start()

                @pl.when(by_y(f))
                def _():
                    first_copy(f, j, row_peer(d)).start()

                @pl.when(straight(f))
                def _():
                    first_copy(f, j, spot_peer(npc - 1 - j)).start()

            @pl.when(jnp.logical_and(by_x(f), jnp.logical_and(j >= ny, j < npc - 1)))
            def _():
                keep[f, j - ny] = total

            @pl.when(jnp.logical_and(by_y(f), j == npc - 2))
            def _():
                keep[f, 0] = total

            @pl.when(mine)
            def _():
                out_ref[pl.ds(f, rows, stride=fields), :] = total

            return carry

        lax.fori_loop(0, npc, one_target, 0)

    def second_step(f):
        @pl.when(by_x(f))
        def _():
            for j in range(ny):
                first_copy(f, j, across).wait_recv()
            for d in range(1, ny):
                part2[f, d - 1] = (keep[f, d - 1] + got1[f, d].astype(F32)).astype(BF)
                second_copy(f, d - 1, row_peer(d)).start()

        @pl.when(by_y(f))
        def _():
            for j in range(npc - 2):
                first_copy(f, j, sibling).wait_recv()
            total = keep[f, 0]
            for j in range(ny - 1):
                total = total + got1[f, j].astype(F32)
            part2[f, 0] = total.astype(BF)
            second_copy(f, 0, across).start()

    def last_step(f):
        at = pl.ds(f, rows, stride=fields)

        @pl.when(by_x(f))
        def _():
            total = out_ref[at, :] + got1[f, 0].astype(F32)
            for j in range(ny - 1):
                second_copy(f, j, sibling).wait_recv()
                total = total + got2[f, j].astype(F32)
            out_ref[at, :] = total

        @pl.when(by_y(f))
        def _():
            total = out_ref[at, :]
            for j in range(ny - 1, npc - 2):
                total = total + got1[f, j].astype(F32)
            second_copy(f, 0, sibling).wait_recv()
            out_ref[at, :] = total + got2[f, 0].astype(F32)

        @pl.when(straight(f))
        def _():
            total = out_ref[at, :]
            for j in range(npc - 1):
                first_copy(f, j, sibling).wait_recv()
                total = total + got1[f, j].astype(F32)
            out_ref[at, :] = total

    def weights_in_plane():
        wa_copy().wait_recv()
        for d in range(1, npc):
            to = (spot + d) % npc
            w1s[to] = (w0[c * npc + to] + wsib[to]).astype(BF)
            w1_copy(d).start()

    def weights_along_z():
        total = w0[c * npc + spot] + wsib[spot]
        for d in range(1, npc):
            w1_copy(d).wait_recv()
            total = total + w1[d].astype(F32)
        w2[z] = total.astype(BF)
        for d in range(1, nz):
            w2_copy(d, z).start()

    def weights_back():
        for d in range(1, nz):
            w2_copy(d, (z + d) % nz).wait_recv()
        total = w2[0].astype(F32)
        for s in range(1, nz):
            total = total + w2[s].astype(F32)
        w3[c * npc + spot] = total.astype(BF)
        for d in range(1, npc):
            w3_copy(d, c * npc + spot).start()

    def weights_to_sibling():
        for d in range(1, npc):
            w3_copy(d, c * npc + (spot - d) % npc).wait_recv()
        wb_copy(c).start()

    for f in range(min(fields, AHEAD)):
        receive(f)

    def one_field(f, carry):
        @pl.when(f + AHEAD < fields)
        def _():
            receive(f + AHEAD)

        field_sums(f)

        for at, step in (
            (0, weights_in_plane), (2, weights_along_z),
            (4, weights_back), (6, weights_to_sibling),
        ):
            @pl.when(f == at)
            def _():
                step()

        @pl.when(f >= LAG_SECOND)
        def _():
            second_step(f - LAG_SECOND)

        @pl.when(f >= LAG_FINAL)
        def _():
            last_step(f - LAG_FINAL)

        return carry

    lax.fori_loop(0, fields, one_field, 0)

    def late_second(f, carry):
        second_step(f)
        return carry

    lax.fori_loop(fields - LAG_SECOND, fields, late_second, 0)
    wb_copy(1 - c).wait_recv()
    wout_ref[...] = w3[...].astype(F32)

    def late_last(f, carry):
        last_step(f)
        return carry

    lax.fori_loop(fields - LAG_FINAL, fields, late_last, 0)

    def drain_z(sent):
        for up in (False, True):
            for hop in (1, 2):
                @pl.when(z_reaches(up, hop))
                def _():
                    sent(z, up, hop).wait_send()
            for o in range(2, nz - 1):
                s = z - o if up else z + o

                @pl.when(jnp.logical_and(z_reaches(up), s >= 0 if up else s < nz))
                def _():
                    sent(s, up, 1).wait_send()

    drain_z(m_copy)
    for s in range(nz):
        ms_copy(s).wait_send()

    def drain(f, carry):
        drain_z(lambda s, up, hop: z_copy(f, s, up, hop))
        for s in range(nz):
            s_copy(f, s).wait_send()

        @pl.when(by_x(f))
        def _():
            for j in range(ny):
                first_copy(f, j, across).wait_send()
            for j in range(ny - 1):
                second_copy(f, j, across).wait_send()

        @pl.when(by_y(f))
        def _():
            for j in range(npc - 2):
                first_copy(f, j, across).wait_send()
            second_copy(f, 0, across).wait_send()

        @pl.when(straight(f))
        def _():
            for j in range(npc - 1):
                first_copy(f, j, across).wait_send()

        return carry

    lax.fori_loop(0, fields, drain, 0)
    wa_copy().wait_send()
    wb_copy(c).wait_send()
    for d in range(1, nz):
        w2_copy(d, z).wait_send()
    for d in range(1, npc):
        w1_copy(d).wait_send()
        w3_copy(d, c * npc + spot).wait_send()


def on_device(size_gx, size_gy, pooled, cotangent, bilinear, bag_ids, bag_lens, row_home):
    samples, fields, width = pooled.shape
    bag = bag_ids.shape[2]
    rows = row_home.shape[1] // (size_gx * size_gy)
    nz, ny, plane = size_gx // 2, size_gy // 2, 2 * size_gy
    npc = 2 * ny
    pairs = fields * (fields - 1) // 2
    piece = (fields - 1) * width // plane
    nb1, nb2 = npc - 1, ny - 1
    vmem = pl.BlockSpec(memory_space=pltpu.VMEM)
    hbm = pl.BlockSpec(memory_space=pltpu.HBM)
    dma = pltpu.SemaphoreType.DMA
    buffers = [
        ((samples, fields, width), BF),
        ((pairs, samples, width), BF),
        ((fields - 1, width, width), BF),
        ((fields, bag, samples), jnp.int32),
        ((fields, samples), jnp.int32),
        (row_home.shape, jnp.int32),
        ((samples * fields, width), F32),
        ((fields - 1, samples, width), F32),
        ((2, nz, fields, bag, samples), jnp.int32),
        ((fields, 2, nz, samples, width), BF),
        ((fields, nb2, rows, width), F32),
        ((fields, nb1, rows, width), BF),
        ((fields, nb1, rows, width), BF),
        ((fields, nb2, rows, width), BF),
        ((fields, nb2, rows, width), BF),
        ((plane, piece, width), F32),
        ((npc, piece, width), F32),
        ((npc, piece, width), BF),
        ((npc, piece, width), BF),
        ((nz, piece, width), BF),
        ((plane, piece, width), BF),
    ]
    held = sum(math.prod(shape) * jnp.dtype(kind).itemsize for shape, kind in buffers)
    table, weight = pl.pallas_call(
        functools.partial(kernel, size_gx, size_gy),
        out_shape=(
            jax.ShapeDtypeStruct((rows * fields, width), F32),
            jax.ShapeDtypeStruct((plane, piece, width), F32),
        ),
        in_specs=[hbm] * 6,
        out_specs=(vmem,) * 2,
        scratch_shapes=[pltpu.VMEM(shape, kind) for shape, kind in buffers] + [
            dma((5,)),
            dma((fields - 1,)),
            dma((5, nz)),
            dma((2, nz)),
            dma((4, fields * nz)),
            dma((fields * nz,)),
            dma((fields * nz,)),
            dma((fields * nz,)),
            dma((fields, nb1)),
            dma((fields, nb1)),
            dma((fields, nb2)),
            dma((fields, nb2)),
            dma((1,)),
            dma((1,)),
            dma((npc,)),
            dma((npc,)),
            dma((nz,)),
            dma((nz,)),
            dma((npc,)),
            dma((npc,)),
            dma((1,)),
            dma((1,)),
        ],
        compiler_params=pltpu.CompilerParams(
            collective_id=0, has_side_effects=True, vmem_limit_bytes=held + (10 << 20)
        ),
    )(*(pltpu.with_memory_space_constraint(v, pltpu.HBM) for v in (
        pooled, cotangent.transpose(1, 0, 2), bilinear,
        bag_ids.transpose(1, 2, 0), bag_lens.transpose(1, 0), row_home,
    )))
    return (
        weight.reshape(fields - 1, width, width),
        table.reshape(rows, fields, width),
    )


def solution(mesh):
    placed = (
        P(("gx", "gy"), None, None),
        P(("gx", "gy"), None, None),
        P(),
        P(("gx", "gy"), None, None),
        P(("gx", "gy"), None),
        P(),
    )
    return jax.shard_map(
        functools.partial(on_device, mesh.shape["gx"], mesh.shape["gy"]),
        mesh=mesh,
        in_specs=placed,
        out_specs=(P(), P(("gx", "gy"), None, None)),
        check_vma=False,
    )
```

time: 59.4 us -> 50.5 us (0.85)
  Pallas kernels: 54.4 us -> 47.9 us
  local copies, waits for them, and re-layouts: 4.08 us -> 1.74 us
    pallas_call x1, Pallas kernels: 54.4 us -> 47.9 us  [on_device(): pl.pallas_call(functools.partial(kernel, size_gx, size_gy), out_shape=(ja...]
    unnamed x2, local copies, waits for them, and re-layouts: 4.08 us -> 1.74 us
where the time goes in v1:
time: 50.5 us; the launch traced here: 50.3 us
  Pallas kernels  47.9 us (95%)
  local copies, waits for them, and re-layouts  1.74 us (3%)
  between operations  0.64 us (1%)
    pallas_call x1, Pallas kernels, on_device(): pl.pallas_call(functools.partial(kernel, size_gx, size_gy), out_shape=(ja...  47.9 us
    unnamed x2, local copies, waits for them, and re-layouts  1.74 us

profile of v1, /device:TPU:0, one launch (start us, length us, event | category | flops | bytes accessed | tf_op | source)
XLA Modules:
  0.0 50.3 jit_solution(18032370078009543573)
XLA Ops:
  0.6 47.9 %shard_map.77 = (f32[2048,128]{1,0:T(8,128)S(1)}, f32[8,112,128]{2,1,0:T(8,128)S(1)}) custom-call(bf16[128,8,128]{2,1,0:T(8,128)(2,1)} %pooled_hbm.1, bf16[28,128,128]{2,1,0:T(8,128)(2,1)} %bitcast.7, bf16[7,128,128]{2,1,0:T(8,128)(2,1)} %bil_hbm.1, s32[8,4,128]{2,1,0:T(4,128)} %bitcast.8, s32[8,128]{1,0:T(8,128)} %bitcast.9, s32[8,8192]{1,0:T(8,128)} %home_hbm.1), custom_call_target="tpu_custom_call" | custom-call | tf_op jit(solution)/shard_map/pallas_call | solution.py:549
  48.6 0.8 %copy.10 = f32[7,128,128]{2,1,0:T(8,128)} copy(f32[7,128,128]{2,1,0:T(8,128)S(1)} %bitcast.6) | data formatting | bytes 917504
  49.3 1.0 %copy.11 = f32[256,8,128]{2,1,0:T(8,128)} copy(f32[256,8,128]{2,1,0:T(8,128)S(1)} %bitcast.5) | data formatting | bytes 2097152

commit v2 on v1

v2 whole, which is shorter than its diff:
```python
import functools
import math

import jax
import jax.numpy as jnp
from jax import lax
from jax.experimental import pallas as pl
from jax.experimental.pallas import tpu as pltpu
from jax.sharding import PartitionSpec as P

MESH = pl.DeviceIdType.MESH
BF = jnp.bfloat16
F32 = jnp.float32
LANES = 128
GROUP = 4
EARLY = 2
W1 = -2
W2 = 0
W3 = 3
W4 = 5
W5 = 7
AHEAD_END = 1
AHEAD_MID = 2
DIRECT = 1
LAG_SECOND = 3
LAG_FINAL = 5


def pair_list(fields):
    return [(i, j) for i in range(fields) for j in range(i + 1, fields)]


def kernel(
    size_gx, size_gy,
    pooled_hbm, cot_hbm, bil_hbm, bag_hbm, lens_hbm, home_hbm,
    out_ref, wout_ref,
    pooled_ref, cot_ref, bil_ref, bag_ref, lens_ref, home_ref,
    pool_f, proj_f, upper_b,
    notes, gath, sums, keep, part1, got1, part2, got2,
    w0, wsib, w1s, w1, w2f, w2s, w2, wz, w3,
    ls, cs,
    ms, mr, zs, zr, ss, sr, p1s, p1r, p2s, p2r,
    was, war, w1ss, w1rs, w2ss, w2rs, wzss, wzrs, w3ss, w3rs, wbs, wbr,
):
    samples, fields, width = pooled_ref.shape
    bag = bag_ref.shape[1]
    rows = keep.shape[2]
    part1_of, part2_of = part1.shape[0] // fields, part2.shape[0] // fields
    nz, ny = size_gx // 2, size_gy // 2
    npc = 2 * ny
    gx, gy = lax.axis_index("gx"), lax.axis_index("gy")
    z, x, y, c = gx // 2, gx % 2, gy // 2, gy % 2
    spot = x * ny + y
    sibling = (gx, y * 2 + 1 - c)
    across = (z * 2 + 1 - x, gy)

    def spot_peer(d):
        to = (spot + d) % npc
        return (z * 2 + to // ny, (to % ny) * 2 + c)

    def row_peer(d):
        return (gx, ((y + d) % ny) * 2 + c)

    def far_peer(d):
        return (z * 2 + 1 - x, ((y + d) % ny) * 2 + c)

    def z_peer(d):
        return (((z + d) % nz) * 2 + x, gy)

    def z_side(up, hop=1):
        return ((z + hop if up else z - hop) * 2 + x, gy)

    def z_reaches(up, hop=1):
        return z < nz - hop if up else z >= hop

    def z_forwards(up):
        return jnp.logical_and(z_reaches(up), z >= 2 if up else z < nz - 2)

    def remote(src, dst, send, recv, dev):
        return pltpu.make_async_remote_copy(
            src_ref=src, dst_ref=dst, send_sem=send, recv_sem=recv,
            device_id=dev, device_id_type=MESH,
        )

    def m_copy(d, slot):
        return remote(notes.at[0, z], notes.at[0, slot], ms.at[0], mr.at[slot], z_peer(d))

    def ms_copy(s):
        return remote(notes.at[0, s], notes.at[1, s], ms.at[1], mr.at[nz], sibling)

    def z_copy(f, s, up, hop=1):
        kind = 0 if hop == 2 else 1 + jnp.where(s == z, 0, 1)
        return remote(
            gath.at[f, 0, s], gath.at[f, 0, s], zs.at[int(up), kind], zr.at[f * nz + s],
            z_side(up, hop),
        )

    def s_copy(f, s):
        return remote(gath.at[f, 0, s], gath.at[f, 1, s], ss.at[0], sr.at[f], sibling)

    def s_copies(f):
        return remote(gath.at[f, 0], gath.at[f, 1], ss.at[0], sr.at[f], sibling)

    def first_copy(f, j, dev):
        at = f * part1_of + j
        return remote(part1.at[at], got1.at[at], p1s.at[0], p1r.at[at], dev)

    def second_copy(f, j, dev):
        at = f * part2_of + j
        return remote(part2.at[at], got2.at[at], p2s.at[0], p2r.at[at], dev)

    def wa_copy():
        return remote(w0.at[pl.ds((1 - c) * npc, npc)], wsib, was.at[0], war.at[0], sibling)

    def w1_copy(d):
        return remote(w1s.at[(spot + d) % npc], w1.at[d], w1ss.at[d], w1rs.at[d], spot_peer(d))

    def w2_copy(d):
        return remote(w2s.at[(z + d) % nz], w2.at[d], w2ss.at[d], w2rs.at[d], z_peer(d))

    def wz_copy(d, slot):
        return remote(wz.at[z], wz.at[slot], wzss.at[d], wzrs.at[d], z_peer(d))

    def w3_copy(d, slot):
        return remote(
            w3.at[c * npc + spot], w3.at[slot], w3ss.at[d], w3rs.at[d], spot_peer(d)
        )

    def wb_copy(half):
        at = pl.ds(half * npc, npc)
        return remote(w3.at[at], w3.at[at], wbs.at[0], wbr.at[0], sibling)

    pairs = pair_list(fields)
    number = {pair: p for p, pair in enumerate(pairs)}
    first = [number[i, i + 1] for i in range(fields - 1)]

    def cot_load(i):
        at = pl.ds(first[i], fields - 1 - i)
        return pltpu.make_async_copy(cot_hbm.at[at], cot_ref.at[at], cs.at[i])

    loads = [
        pltpu.make_async_copy(src, dst, ls.at[n])
        for n, (src, dst) in enumerate([
            (pooled_hbm, pooled_ref), (bil_hbm, bil_ref), (bag_hbm, bag_ref),
            (lens_hbm, lens_ref), (home_hbm, home_ref),
        ])
    ]
    for n in (4, 2, 3, 0):
        loads[n].start()
    cot_load(0).start()
    loads[1].start()
    for i in range(1, fields - 1):
        cot_load(i).start()

    barrier = pltpu.get_barrier_semaphore()
    for d in range(1, nz):
        pl.semaphore_signal(barrier, inc=1, device_id=z_peer(d), device_id_type=MESH)
    for d in range(1, npc):
        pl.semaphore_signal(barrier, inc=1, device_id=spot_peer(d), device_id_type=MESH)
    pl.semaphore_signal(barrier, inc=1, device_id=sibling, device_id_type=MESH)

    def spread_out(b, carry):
        pool_f[pl.ds(pl.multiple_of(b * fields, fields), fields), :] = pooled_ref[b].astype(F32)
        return carry

    def write_notes():
        for load in loads[2:]:
            load.wait()
        bags = [bag_ref[:, k, :] for k in range(bag)]
        high = [b // LANES for b in bags]
        low = [b % LANES for b in bags]

        def look(h, found):
            row = home_ref[:, pl.ds(pl.multiple_of(h * LANES, LANES), LANES)]
            return tuple(
                jnp.where(high[k] == h, jnp.take_along_axis(row, low[k], axis=1), found[k])
                for k in range(bag)
            )

        none = jnp.full(lens_ref.shape, 0, jnp.int32)
        found = lax.fori_loop(0, home_ref.shape[1] // LANES, look, (none,) * bag, unroll=64)
        lens = lens_ref[...]
        live = [jnp.where(lens > k, found[k], -1) for k in range(bag)]
        for k in range(bag):
            times = None
            for other in live:
                same = jnp.where(live[k] == other, 1, 0)
                times = same if times is None else times + same
            notes[0, z, :, k, :] = live[k] * 8 + jnp.where(live[k] < 0, 0, times)

    write_notes()
    loads[0].wait()
    lax.fori_loop(0, samples, spread_out, 0, unroll=8)
    loads[1].wait()

    pool = lambda f: pool_f[pl.ds(f, samples, stride=fields), :]
    cot = lambda i, j: cot_ref[number[i, j]].astype(F32)
    piece, share = w0.shape[1], wz.shape[1]

    def send_own(copy, early=True):
        for hop in (2, 1):
            for up in (False, True):
                ok = z_reaches(up, hop)
                if hop == 1 and not early:
                    ok = jnp.logical_and(ok, jnp.logical_not(z_forwards(up)))

                @pl.when(ok)
                def _():
                    copy(up, hop).start()

    for i in range(fields):
        total = None
        if i < fields - 1:
            cot_load(i).wait()
            mine = pool(i).astype(BF)
            upper = jnp.zeros((samples, width), F32)
            for j in range(i + 1, fields):
                upper = upper + cot(i, j) * pool(j)
            upper = upper.astype(BF)
            total = lax.dot_general(
                upper, bil_ref[i], (((1,), (1,)), ((), ())), preferred_element_type=F32
            )
        for k in range(i):
            term = cot(k, i) * proj_f[k]
            total = term if total is None else total + term
        gath[i, 0, z] = total.astype(BF)
        if i == 0:
            pl.semaphore_wait(barrier, nz - 1 + npc - 1 + 1)
            for d in range(1, nz):
                m_copy(d, z).start()
            ms_copy(z).start()
        send_own(lambda up, hop: z_copy(i, z, up, hop), i < EARLY)
        s_copy(i, z).start()
        if i < fields - 1:
            upper_b[i] = upper
            proj_f[i] = jnp.dot(mine, bil_ref[i], preferred_element_type=F32)

    def weights_here():
        for i in range(fields - 1):
            wide_w = lax.dot_general(
                pool(i).astype(BF), upper_b[i], (((0,), (0,)), ((), ())),
                preferred_element_type=F32,
            )
            at, end = i * width, (i + 1) * width
            while at < end:
                p, r = at // piece, at % piece
                n = min(piece - r, end - at)
                w0[p, r : r + n, :] = wide_w[at - i * width : at - i * width + n, :]
                at += n
        wa_copy().start()

    weights_here()

    def take(arrived, onward, to_sibling):
        for o in range(1, nz):
            for up in (True, False):
                s = z - o if up else z + o

                @pl.when(s >= 0 if up else s < nz)
                def _():
                    arrived(s)

                    if o > 1:
                        @pl.when(z_reaches(up))
                        def _():
                            onward(s, up)

                    to_sibling(s)

    def receive(f):
        take(
            lambda s: z_copy(f, s, True).wait_recv(),
            lambda s, up: z_copy(f, s, up).start(),
            lambda s: s_copy(f, s).start(),
        )
        for up in (False, True):
            @pl.when(jnp.logical_and(z_forwards(up), f + EARLY < fields))
            def _():
                z_copy(f + EARLY, z, up).start()

    for d in range(1, nz):
        s = (z + d) % nz
        m_copy(d, s).wait_recv()
        ms_copy(s).start()

    steps = (
        (W1, lambda: weights_in_plane()), (W2, lambda: weights_along_z()),
        (W3, lambda: weights_back_z()), (W4, lambda: weights_back()),
        (W5, lambda: weights_to_sibling()),
    )

    row_number = lax.broadcasted_iota(jnp.int32, (rows, samples), 0).astype(F32).astype(BF)
    zero = jnp.zeros((), BF)

    def owner_of(t):
        return 1 - x if t // ny == 1 else x, (y + t % ny) % ny

    def add_half(f, core):
        fresh = core == 0
        for t0 in range(0, npc, GROUP):
            totals = [None] * GROUP
            for s in range(0, nz, 2):
                held = jnp.concatenate([gath[f, core, s], gath[f, core, s + 1]], axis=0)
                place = [notes[core, s + e, f] >> 3 for e in range(2)]
                times = [(notes[core, s + e, f] & 7).astype(F32).astype(BF) for e in range(2)]
                for t in range(GROUP):
                    x_to, y_to = owner_of(t0 + t)
                    base = ((z * 2 + x_to) * size_gy + y_to * 2 + c) * rows
                    blocks = []
                    for e in range(2):
                        key = (place[e] - base).astype(F32).astype(BF)
                        count = zero
                        for k in range(bag):
                            count = jnp.where(
                                row_number == key[k : k + 1, :], times[e][k : k + 1, :], count
                            )
                        blocks.append(count)
                    part = jnp.dot(
                        jnp.concatenate(blocks, axis=1), held, preferred_element_type=F32
                    )
                    totals[t] = part if totals[t] is None else totals[t] + part
            for t in range(GROUP):
                sums[t0 + t] = totals[t] if fresh else sums[t0 + t] + totals[t]

    def by_x(f):
        return jnp.logical_and(f % 2 == 0, f < fields - DIRECT)

    def by_y(f):
        return jnp.logical_and(f % 2 == 1, f < fields - DIRECT)

    def straight(f):
        return f >= fields - DIRECT

    def field_sums(f):
        add_half(f, 0)
        s_copies(f).wait_recv()
        add_half(f, 1)

        @pl.when(by_x(f))
        def _():
            for d in range(ny):
                part1[f * part1_of + d] = sums[ny + d].astype(BF)
                first_copy(f, d, across).start()
            for d in range(1, ny):
                keep[f, d - 1] = sums[d]

        @pl.when(by_y(f))
        def _():
            for d in range(1, ny):
                part1[f * part1_of + d - 1] = sums[ny + d].astype(BF)
                first_copy(f, d - 1, row_peer(d)).start()
                part1[f * part1_of + ny + d - 2] = sums[d].astype(BF)
                first_copy(f, ny + d - 2, row_peer(d)).start()
            keep[f, 0] = sums[ny]

        @pl.when(straight(f))
        def _():
            for d in range(ny - 1, -1, -1):
                for other in (1, 0):
                    t = other * ny + d
                    if t:
                        part1[f * part1_of + t - 1] = sums[t].astype(BF)
                        dev = across if d == 0 else row_peer(d) if other == 0 else far_peer(d)
                        first_copy(f, t - 1, dev).start()

        out_ref[pl.ds(f, rows, stride=fields), :] = sums[0]

    def second_step(f):
        @pl.when(by_x(f))
        def _():
            for j in range(ny):
                first_copy(f, j, across).wait_recv()
            for d in range(1, ny):
                part2[f * part2_of + d - 1] = (keep[f, d - 1] + got1[f * part1_of + d].astype(F32)).astype(BF)
                second_copy(f, d - 1, row_peer(d)).start()

        @pl.when(by_y(f))
        def _():
            for j in range(npc - 2):
                first_copy(f, j, sibling).wait_recv()
            total = keep[f, 0]
            for j in range(ny - 1):
                total = total + got1[f * part1_of + j].astype(F32)
            part2[f * part2_of + 0] = total.astype(BF)
            second_copy(f, 0, across).start()

    def last_step(f):
        at = pl.ds(f, rows, stride=fields)

        @pl.when(by_x(f))
        def _():
            total = out_ref[at, :] + got1[f * part1_of + 0].astype(F32)
            for j in range(ny - 1):
                second_copy(f, j, sibling).wait_recv()
                total = total + got2[f * part2_of + j].astype(F32)
            out_ref[at, :] = total

        @pl.when(by_y(f))
        def _():
            total = out_ref[at, :]
            for j in range(ny - 1, npc - 2):
                total = total + got1[f * part1_of + j].astype(F32)
            second_copy(f, 0, sibling).wait_recv()
            out_ref[at, :] = total + got2[f * part2_of + 0].astype(F32)

        @pl.when(straight(f))
        def _():
            total = out_ref[at, :]
            for j in range(npc - 1):
                first_copy(f, j, sibling).wait_recv()
                total = total + got1[f * part1_of + j].astype(F32)
            out_ref[at, :] = total

    def weights_in_plane():
        wa_copy().wait_recv()
        for d in range(1, npc):
            to = (spot + d) % npc
            w1s[to] = (w0[c * npc + to] + wsib[to]).astype(BF)
            w1_copy(d).start()

    def slices(r):
        return slice(min(piece, r * share), min(piece, (r + 1) * share))

    def weights_along_z():
        total = w0[c * npc + spot] + wsib[spot]
        for d in range(1, npc):
            w1_copy(d).wait_recv()
            total = total + w1[d].astype(F32)
        for r in range(-(-piece // share)):
            rows_r = total[slices(r)]
            w2f[r, : rows_r.shape[0]] = rows_r
            w2s[r, : rows_r.shape[0]] = rows_r.astype(BF)
        for d in range(1, nz):
            w2_copy(d).start()

    def weights_back_z():
        total = w2f[z]
        for d in range(1, nz):
            w2_copy(d).wait_recv()
            total = total + w2[d].astype(F32)
        wz[z] = total.astype(BF)
        for d in range(1, nz):
            wz_copy(d, z).start()

    def weights_back():
        for d in range(1, nz):
            wz_copy(d, (z - d) % nz).wait_recv()
        for r in range(-(-piece // share)):
            at = slices(r)
            w3[c * npc + spot, at] = wz[r, : at.stop - at.start]
        for d in range(1, npc):
            w3_copy(d, c * npc + spot).start()

    def weights_to_sibling():
        for d in range(1, npc):
            w3_copy(d, c * npc + (spot - d) % npc).wait_recv()
        wb_copy(c).start()

    def early_steps(n):
        for at, step in steps:
            if at == n:
                step()

    early_steps(-2)
    ahead = jnp.where(jnp.logical_and(z > 0, z < nz - 1), AHEAD_MID, AHEAD_END)
    for f in range(min(fields, max(AHEAD_MID, AHEAD_END))):
        @pl.when(f < ahead)
        def _():
            receive(f)

    early_steps(-1)
    remote(notes.at[0], notes.at[1], ms.at[1], mr.at[nz], sibling).wait_recv()

    def one_field(f, carry):
        @pl.when(f + ahead < fields)
        def _():
            receive(f + ahead)

        field_sums(f)

        for at, step in steps:
            if at >= 0:
                @pl.when(f == at)
                def _():
                    step()

        @pl.when(f >= LAG_SECOND)
        def _():
            second_step(f - LAG_SECOND)

        @pl.when(f >= LAG_FINAL)
        def _():
            last_step(f - LAG_FINAL)

        return carry

    lax.fori_loop(0, fields, one_field, 0)

    def late_second(f, carry):
        second_step(f)
        return carry

    lax.fori_loop(fields - LAG_SECOND, fields, late_second, 0)
    wb_copy(1 - c).wait_recv()
    wout_ref[...] = w3[...].astype(F32)

    def late_last(f, carry):
        last_step(f)
        return carry

    lax.fori_loop(fields - LAG_FINAL, fields, late_last, 0)

    def sent(ref, sem):
        remote(ref, ref, sem, zr.at[0], sibling).wait_send()

    for up in (False, True):
        for hop in (1, 2):
            @pl.when(z_reaches(up, hop))
            def _():
                sent(gath.at[:, 0, 0], zs.at[int(up), 2 - hop])
        for o in range(2, nz - 1):
            @pl.when(jnp.logical_and(z_reaches(up), z >= o if up else z < nz - o))
            def _():
                sent(gath.at[:, 0, 0], zs.at[int(up), 2])
    for d in range(1, nz):
        m_copy(d, z).wait_send()
    sent(notes.at[0], ms.at[1])
    sent(gath.at[:, 0], ss.at[0])
    two_step = range(fields - DIRECT)
    n1 = sum(ny if f % 2 == 0 else npc - 2 for f in two_step) + DIRECT * (npc - 1)
    n2 = sum(ny - 1 if f % 2 == 0 else 1 for f in two_step)
    sent(part1.at[pl.ds(0, n1)], p1s.at[0])
    sent(part2.at[pl.ds(0, n2)], p2s.at[0])
    wa_copy().wait_send()
    wb_copy(c).wait_send()
    for d in range(1, nz):
        w2_copy(d).wait_send()
        wz_copy(d, z).wait_send()
    for d in range(1, npc):
        w1_copy(d).wait_send()
        w3_copy(d, c * npc + spot).wait_send()


def on_device(size_gx, size_gy, pooled, cotangent, bilinear, bag_ids, bag_lens, row_home):
    samples, fields, width = pooled.shape
    bag = bag_ids.shape[2]
    rows = row_home.shape[1] // (size_gx * size_gy)
    nz, ny, plane = size_gx // 2, size_gy // 2, 2 * size_gy
    npc = 2 * ny
    pairs = fields * (fields - 1) // 2
    piece = (fields - 1) * width // plane
    nb1, nb2 = npc - 1, ny - 1
    share = -(-piece // nz)
    vmem = pl.BlockSpec(memory_space=pltpu.VMEM)
    hbm = pl.BlockSpec(memory_space=pltpu.HBM)
    dma = pltpu.SemaphoreType.DMA
    buffers = [
        ((samples, fields, width), BF),
        ((pairs, samples, width), BF),
        ((fields - 1, width, width), BF),
        ((fields, bag, samples), jnp.int32),
        ((fields, samples), jnp.int32),
        (row_home.shape, jnp.int32),
        ((samples * fields, width), F32),
        ((fields - 1, samples, width), F32),
        ((fields - 1, samples, width), BF),
        ((2, nz, fields, bag, samples), jnp.int32),
        ((fields, 2, nz, samples, width), BF),
        ((npc, rows, width), F32),
        ((fields, nb2, rows, width), F32),
        ((fields * nb1, rows, width), BF),
        ((fields * nb1, rows, width), BF),
        ((fields * nb2, rows, width), BF),
        ((fields * nb2, rows, width), BF),
        ((plane, piece, width), F32),
        ((npc, piece, width), F32),
        ((npc, piece, width), BF),
        ((npc, piece, width), BF),
        ((nz, share, width), F32),
        ((nz, share, width), BF),
        ((nz, share, width), BF),
        ((nz, share, width), BF),
        ((plane, piece, width), BF),
    ]
    held = sum(math.prod(shape) * jnp.dtype(kind).itemsize for shape, kind in buffers)
    table, weight = pl.pallas_call(
        functools.partial(kernel, size_gx, size_gy),
        out_shape=(
            jax.ShapeDtypeStruct((rows * fields, width), F32),
            jax.ShapeDtypeStruct((plane, piece, width), F32),
        ),
        in_specs=[hbm] * 6,
        out_specs=(vmem,) * 2,
        scratch_shapes=[pltpu.VMEM(shape, kind) for shape, kind in buffers] + [
            dma((5,)),
            dma((fields - 1,)),
            dma((2,)),
            dma((nz + 1,)),
            dma((2, 3)),
            dma((fields * nz,)),
            dma((1,)),
            dma((fields,)),
            dma((1,)),
            dma((fields * nb1,)),
            dma((1,)),
            dma((fields * nb2,)),
            dma((1,)),
            dma((1,)),
            dma((npc,)),
            dma((npc,)),
            dma((nz,)),
            dma((nz,)),
            dma((nz,)),
            dma((nz,)),
            dma((npc,)),
            dma((npc,)),
            dma((1,)),
            dma((1,)),
        ],
        compiler_params=pltpu.CompilerParams(
            collective_id=0, has_side_effects=True, vmem_limit_bytes=held + (10 << 20)
        ),
    )(*(pltpu.with_memory_space_constraint(v, pltpu.HBM) for v in (
        pooled, cotangent.transpose(1, 0, 2), bilinear,
        bag_ids.transpose(1, 2, 0), bag_lens.transpose(1, 0), row_home,
    )))
    return (
        weight.reshape(fields - 1, width, width),
        table.reshape(rows, fields, width),
    )


def solution(mesh):
    placed = (
        P(("gx", "gy"), None, None),
        P(("gx", "gy"), None, None),
        P(),
        P(("gx", "gy"), None, None),
        P(("gx", "gy"), None),
        P(),
    )
    return jax.shard_map(
        functools.partial(on_device, mesh.shape["gx"], mesh.shape["gy"]),
        mesh=mesh,
        in_specs=placed,
        out_specs=(P(), P(("gx", "gy"), None, None)),
        check_vma=False,
    )
```

time: 50.5 us -> 48.7 us (0.964)
  Pallas kernels: 47.9 us -> 46.2 us
    pallas_call x1, Pallas kernels: 47.9 us -> 46.2 us  [on_device(): pl.pallas_call(functools.partial(kernel, size_gx, size_gy), out_shape=(ja...]
where the time goes in v2:
time: 48.7 us; the launch traced here: 48.5 us
  Pallas kernels  46.2 us (95%)
  local copies, waits for them, and re-layouts  1.74 us (4%)
  between operations  0.64 us (1%)
    pallas_call x1, Pallas kernels, on_device(): pl.pallas_call(functools.partial(kernel, size_gx, size_gy), out_shape=(ja...  46.2 us
    unnamed x2, local copies, waits for them, and re-layouts  1.74 us

profile of v2, /device:TPU:0, one launch (start us, length us, event | category | flops | bytes accessed | tf_op | source)
XLA Modules:
  0.0 48.5 jit_solution(12284962419145264485)
XLA Ops:
  0.6 46.2 %shard_map.77 = (f32[2048,128]{1,0:T(8,128)S(1)}, f32[8,112,128]{2,1,0:T(8,128)S(1)}) custom-call(bf16[128,8,128]{2,1,0:T(8,128)(2,1)} %pooled_hbm.1, bf16[28,128,128]{2,1,0:T(8,128)(2,1)} %bitcast.7, bf16[7,128,128]{2,1,0:T(8,128)(2,1)} %bil_hbm.1, s32[8,4,128]{2,1,0:T(4,128)} %bitcast.8, s32[8,128]{1,0:T(8,128)} %bitcast.9, s32[8,8192]{1,0:T(8,128)} %home_hbm.1), custom_call_target="tpu_custom_call" | custom-call | tf_op jit(solution)/shard_map/pallas_call | solution.py:586
  46.8 0.8 %copy.10 = f32[7,128,128]{2,1,0:T(8,128)} copy(f32[7,128,128]{2,1,0:T(8,128)S(1)} %bitcast.6) | data formatting | bytes 917504
  47.6 1.0 %copy.11 = f32[256,8,128]{2,1,0:T(8,128)} copy(f32[256,8,128]{2,1,0:T(8,128)S(1)} %bitcast.5) | data formatting | bytes 2097152

commit v3 on v2

--- a/solution.py
+++ b/solution.py
@@ -12,18 +12,20 @@
 BF = jnp.bfloat16
 F32 = jnp.float32
 LANES = 128
+PLANE = 1
+PLANE_AT = 6
 GROUP = 4
 EARLY = 2
 W1 = -2
-W2 = 0
+W2 = 1
 W3 = 3
 W4 = 5
 W5 = 7
-AHEAD_END = 1
+AHEAD_END = 0
 AHEAD_MID = 2
 DIRECT = 1
-LAG_SECOND = 3
-LAG_FINAL = 5
+LAG_SECOND = 2
+LAG_FINAL = 8
 
 
 def pair_list(fields):
@@ -36,10 +38,10 @@
     out_ref, wout_ref,
     pooled_ref, cot_ref, bil_ref, bag_ref, lens_ref, home_ref,
     pool_f, proj_f, upper_b,
-    notes, gath, sums, keep, part1, got1, part2, got2,
+    notes, notes_p, gath, gath_p, part_z, got_z, sums, keep, part1, got1, part2, got2,
     w0, wsib, w1s, w1, w2f, w2s, w2, wz, w3,
     ls, cs,
-    ms, mr, zs, zr, ss, sr, p1s, p1r, p2s, p2r,
+    ms, mr, ns, nr, gs, gr, hs, hr, zs, zr, ss, sr, p1s, p1r, p2s, p2r,
     was, war, w1ss, w1rs, w2ss, w2rs, wzss, wzrs, w3ss, w3rs, wbs, wbr,
 ):
     samples, fields, width = pooled_ref.shape
@@ -88,18 +90,39 @@
     def ms_copy(s):
         return remote(notes.at[0, s], notes.at[1, s], ms.at[1], mr.at[nz], sibling)
 
+    def n_copy(d, slot):
+        return remote(notes_p.at[0, spot], notes_p.at[0, slot], ns.at[0], nr.at[slot], spot_peer(d))
+
+    def ns_copy(s):
+        return remote(notes_p.at[0, s], notes_p.at[1, s], ns.at[1], nr.at[npc], sibling)
+
+    def g_copy(f, d, slot):
+        return remote(
+            gath_p.at[f, 0, spot], gath_p.at[f, 0, slot], gs.at[0], gr.at[f * npc + slot],
+            spot_peer(d),
+        )
+
+    def gs_copy(f, s):
+        return remote(
+            gath_p.at[f, 0, s], gath_p.at[f, 1, s], gs.at[1], gr.at[PLANE * npc + f], sibling
+        )
+
+    def h_copy(f, d):
+        at = f * (nz - 1) + d - 1
+        return remote(part_z.at[at], got_z.at[at], hs.at[0], hr.at[at], z_peer(d))
+
     def z_copy(f, s, up, hop=1):
         kind = 0 if hop == 2 else 1 + jnp.where(s == z, 0, 1)
         return remote(
-            gath.at[f, 0, s], gath.at[f, 0, s], zs.at[int(up), kind], zr.at[f * nz + s],
+            gath.at[f - PLANE, 0, s], gath.at[f - PLANE, 0, s], zs.at[int(up), kind], zr.at[f * nz + s],
             z_side(up, hop),
         )
 
     def s_copy(f, s):
-        return remote(gath.at[f, 0, s], gath.at[f, 1, s], ss.at[0], sr.at[f], sibling)
+        return remote(gath.at[f - PLANE, 0, s], gath.at[f - PLANE, 1, s], ss.at[0], sr.at[f], sibling)
 
     def s_copies(f):
-        return remote(gath.at[f, 0], gath.at[f, 1], ss.at[0], sr.at[f], sibling)
+        return remote(gath.at[f - PLANE, 0], gath.at[f - PLANE, 1], ss.at[0], sr.at[f], sibling)
 
     def first_copy(f, j, dev):
         at = f * part1_of + j
@@ -186,7 +209,9 @@
             for other in live:
                 same = jnp.where(live[k] == other, 1, 0)
                 times = same if times is None else times + same
-            notes[0, z, :, k, :] = live[k] * 8 + jnp.where(live[k] < 0, 0, times)
+            note = live[k] * 8 + jnp.where(live[k] < 0, 0, times)
+            notes[0, z, :, k, :] = note
+            notes_p[0, spot, :, k, :] = note[:PLANE]
 
     write_notes()
     loads[0].wait()
@@ -223,14 +248,25 @@
         for k in range(i):
             term = cot(k, i) * proj_f[k]
             total = term if total is None else total + term
-        gath[i, 0, z] = total.astype(BF)
+        if i < PLANE:
+            gath_p[i, 0, spot] = total.astype(BF)
+        else:
+            gath[i - PLANE, 0, z] = total.astype(BF)
         if i == 0:
             pl.semaphore_wait(barrier, nz - 1 + npc - 1 + 1)
             for d in range(1, nz):
                 m_copy(d, z).start()
             ms_copy(z).start()
-        send_own(lambda up, hop: z_copy(i, z, up, hop), i < EARLY)
-        s_copy(i, z).start()
+            for d in range(1, npc):
+                n_copy(d, spot).start()
+            ns_copy(spot).start()
+        if i < PLANE:
+            for d in range(npc - 1, 0, -1):
+                g_copy(i, d, spot).start()
+            gs_copy(i, spot).start()
+        else:
+            send_own(lambda up, hop: z_copy(i, z, up, hop), i < PLANE + EARLY)
+            s_copy(i, z).start()
         if i < fields - 1:
             upper_b[i] = upper
             proj_f[i] = jnp.dot(mine, bil_ref[i], preferred_element_type=F32)
@@ -278,6 +314,13 @@
             def _():
                 z_copy(f + EARLY, z, up).start()
 
+    for d in range(1, npc):
+        s = (spot + d) % npc
+        n_copy(d, s).wait_recv()
+        ns_copy(s).start()
+        for f in range(PLANE):
+            g_copy(f, d, s).wait_recv()
+            gs_copy(f, s).start()
     for d in range(1, nz):
         s = (z + d) % nz
         m_copy(d, s).wait_recv()
@@ -295,17 +338,18 @@
     def owner_of(t):
         return 1 - x if t // ny == 1 else x, (y + t % ny) % ny
 
-    def add_half(f, core):
-        fresh = core == 0
-        for t0 in range(0, npc, GROUP):
-            totals = [None] * GROUP
-            for s in range(0, nz, 2):
-                held = jnp.concatenate([gath[f, core, s], gath[f, core, s + 1]], axis=0)
-                place = [notes[core, s + e, f] >> 3 for e in range(2)]
-                times = [(notes[core, s + e, f] & 7).astype(F32).astype(BF) for e in range(2)]
-                for t in range(GROUP):
-                    x_to, y_to = owner_of(t0 + t)
-                    base = ((z * 2 + x_to) * size_gy + y_to * 2 + c) * rows
+    def add_half(values, note_of, sources, owners, fresh):
+        group = min(GROUP, len(owners))
+        for t0 in range(0, len(owners), group):
+            totals = [None] * group
+            for s in range(0, sources, 2):
+                held = jnp.concatenate([values(s), values(s + 1)], axis=0)
+                note = [note_of(s), note_of(s + 1)]
+                place = [n >> 3 for n in note]
+                times = [(n & 7).astype(F32).astype(BF) for n in note]
+                for t in range(group):
+                    z_to, x_to, y_to = owners[t0 + t]
+                    base = ((z_to * 2 + x_to) * size_gy + y_to * 2 + c) * rows
                     blocks = []
                     for e in range(2):
                         key = (place[e] - base).astype(F32).astype(BF)
@@ -319,8 +363,31 @@
                         jnp.concatenate(blocks, axis=1), held, preferred_element_type=F32
                     )
                     totals[t] = part if totals[t] is None else totals[t] + part
-            for t in range(GROUP):
+            for t in range(group):
                 sums[t0 + t] = totals[t] if fresh else sums[t0 + t] + totals[t]
+
+    def plane_sums(f):
+        owners = [((z + d) % nz, x, y) for d in range(nz)]
+        for core in range(2):
+            if core:
+                remote(
+                    gath_p.at[f, 0], gath_p.at[f, 1], gs.at[1], gr.at[PLANE * npc + f], sibling
+                ).wait_recv()
+            add_half(
+                lambda s: gath_p[f, core, s], lambda s: notes_p[core, s, f], npc, owners,
+                core == 0,
+            )
+        for d in range(1, nz):
+            part_z[f * (nz - 1) + d - 1] = sums[d].astype(BF)
+        out_ref[pl.ds(f, rows, stride=fields), :] = sums[0]
+
+    def plane_last(f):
+        at = pl.ds(f, rows, stride=fields)
+        total = out_ref[at, :]
+        for d in range(1, nz):
+            h_copy(f, d).wait_recv()
+            total = total + got_z[f * (nz - 1) + d - 1].astype(F32)
+        out_ref[at, :] = total
 
     def by_x(f):
         return jnp.logical_and(f % 2 == 0, f < fields - DIRECT)
@@ -332,9 +399,14 @@
         return f >= fields - DIRECT
 
     def field_sums(f):
-        add_half(f, 0)
-        s_copies(f).wait_recv()
-        add_half(f, 1)
+        owners = [(z, *owner_of(t)) for t in range(npc)]
+        for core in range(2):
+            if core:
+                s_copies(f).wait_recv()
+            add_half(
+                lambda s: gath[f - PLANE, core, s], lambda s: notes[core, s, f], nz, owners,
+                core == 0,
+            )
 
         @pl.when(by_x(f))
         def _():
@@ -462,17 +534,28 @@
                 step()
 
     early_steps(-2)
-    ahead = jnp.where(jnp.logical_and(z > 0, z < nz - 1), AHEAD_MID, AHEAD_END)
-    for f in range(min(fields, max(AHEAD_MID, AHEAD_END))):
+    if PLANE:
+        remote(notes_p.at[0], notes_p.at[1], ns.at[1], nr.at[npc], sibling).wait_recv()
+    for f in range(PLANE):
+        plane_sums(f)
+    edge = jnp.logical_or(z == 0, z == nz - 1)
+    ahead = jnp.where(edge, AHEAD_END, AHEAD_MID)
+    for f in range(max(AHEAD_MID, AHEAD_END)):
         @pl.when(f < ahead)
         def _():
-            receive(f)
+            receive(PLANE + f)
 
     early_steps(-1)
     remote(notes.at[0], notes.at[1], ms.at[1], mr.at[nz], sibling).wait_recv()
 
     def one_field(f, carry):
-        @pl.when(f + ahead < fields)
+        held_back = jnp.logical_and(edge, f == PLANE) if AHEAD_END else f < 0
+        if AHEAD_END:
+            @pl.when(jnp.logical_and(edge, f == PLANE + 1))
+            def _():
+                receive(f + AHEAD_END - 1)
+
+        @pl.when(jnp.logical_and(f + ahead < fields, jnp.logical_not(held_back)))
         def _():
             receive(f + ahead)
 
@@ -484,23 +567,31 @@
                 def _():
                     step()
 
-        @pl.when(f >= LAG_SECOND)
+        @pl.when(f == PLANE_AT)
+        def _():
+            for k in range(PLANE):
+                for d in range(1, nz):
+                    h_copy(k, d).start()
+
+        @pl.when(f >= PLANE + LAG_SECOND)
         def _():
             second_step(f - LAG_SECOND)
 
-        @pl.when(f >= LAG_FINAL)
+        @pl.when(f >= PLANE + LAG_FINAL)
         def _():
             last_step(f - LAG_FINAL)
 
         return carry
 
-    lax.fori_loop(0, fields, one_field, 0)
+    lax.fori_loop(PLANE, fields, one_field, 0)
 
     def late_second(f, carry):
         second_step(f)
         return carry
 
-    lax.fori_loop(fields - LAG_SECOND, fields, late_second, 0)
+    lax.fori_loop(max(PLANE, fields - LAG_SECOND), fields, late_second, 0)
+    for f in range(PLANE):
+        plane_last(f)
     wb_copy(1 - c).wait_recv()
     wout_ref[...] = w3[...].astype(F32)
 
@@ -508,7 +599,7 @@
         last_step(f)
         return carry
 
-    lax.fori_loop(fields - LAG_FINAL, fields, late_last, 0)
+    lax.fori_loop(max(PLANE, fields - LAG_FINAL), fields, late_last, 0)
 
     def sent(ref, sem):
         remote(ref, ref, sem, zr.at[0], sibling).wait_send()
@@ -526,9 +617,17 @@
         m_copy(d, z).wait_send()
     sent(notes.at[0], ms.at[1])
     sent(gath.at[:, 0], ss.at[0])
-    two_step = range(fields - DIRECT)
+    two_step = range(PLANE, fields - DIRECT)
     n1 = sum(ny if f % 2 == 0 else npc - 2 for f in two_step) + DIRECT * (npc - 1)
     n2 = sum(ny - 1 if f % 2 == 0 else 1 for f in two_step)
+    if PLANE:
+        for d in range(1, npc):
+            n_copy(d, spot).wait_send()
+            for f in range(PLANE):
+                g_copy(f, d, spot).wait_send()
+        sent(notes_p.at[0], ns.at[1])
+        sent(gath_p.at[:, 0], gs.at[1])
+        sent(part_z, hs.at[0])
     sent(part1.at[pl.ds(0, n1)], p1s.at[0])
     sent(part2.at[pl.ds(0, n2)], p2s.at[0])
     wa_copy().wait_send()
@@ -565,8 +664,12 @@
         ((fields - 1, samples, width), F32),
         ((fields - 1, samples, width), BF),
         ((2, nz, fields, bag, samples), jnp.int32),
-        ((fields, 2, nz, samples, width), BF),
-        ((npc, rows, width), F32),
+        ((2, npc, PLANE, bag, samples), jnp.int32),
+        ((fields - PLANE, 2, nz, samples, width), BF),
+        ((PLANE, 2, npc, samples, width), BF),
+        ((PLANE * (nz - 1), rows, width), BF),
+        ((PLANE * (nz - 1), rows, width), BF),
+        ((max(npc, nz), rows, width), F32),
         ((fields, nb2, rows, width), F32),
         ((fields * nb1, rows, width), BF),
         ((fields * nb1, rows, width), BF),
@@ -596,6 +699,12 @@
             dma((fields - 1,)),
             dma((2,)),
             dma((nz + 1,)),
+            dma((2,)),
+            dma((npc + 1,)),
+            dma((2,)),
+            dma((PLANE * npc + PLANE,)),
+            dma((1,)),
+            dma((PLANE * (nz - 1),)),
             dma((2, 3)),
             dma((fields * nz,)),
             dma((1,)),

time: 48.7 us -> 45.2 us (0.928)
  Pallas kernels: 46.2 us -> 42.7 us
    pallas_call x1, Pallas kernels: 46.2 us -> 42.7 us  [on_device(): pl.pallas_call(functools.partial(kernel, size_gx, size_gy), out_shape=(ja...]
where the time goes in v3:
time: 45.2 us; the launch traced here: 45 us
  Pallas kernels  42.7 us (94%)
  local copies, waits for them, and re-layouts  1.74 us (4%)
  between operations  0.64 us (1%)
    pallas_call x1, Pallas kernels, on_device(): pl.pallas_call(functools.partial(kernel, size_gx, size_gy), out_shape=(ja...  42.7 us
    unnamed x2, local copies, waits for them, and re-layouts  1.74 us

profile of v3, /device:TPU:0, one launch (start us, length us, event | category | flops | bytes accessed | tf_op | source)
XLA Modules:
  0.0 45.0 jit_solution(5836667740063917141)
XLA Ops:
  0.6 42.7 %shard_map.77 = (f32[2048,128]{1,0:T(8,128)S(1)}, f32[8,112,128]{2,1,0:T(8,128)S(1)}) custom-call(bf16[128,8,128]{2,1,0:T(8,128)(2,1)} %pooled_hbm.1, bf16[28,128,128]{2,1,0:T(8,128)(2,1)} %bitcast.7, bf16[7,128,128]{2,1,0:T(8,128)(2,1)} %bil_hbm.1, s32[8,4,128]{2,1,0:T(4,128)} %bitcast.8, s32[8,128]{1,0:T(8,128)} %bitcast.9, s32[8,8192]{1,0:T(8,128)} %home_hbm.1), custom_call_target="tpu_custom_call" | custom-call | tf_op jit(solution)/shard_map/pallas_call | solution.py:689
  43.3 0.8 %copy.10 = f32[7,128,128]{2,1,0:T(8,128)} copy(f32[7,128,128]{2,1,0:T(8,128)S(1)} %bitcast.6) | data formatting | bytes 917504
  44.1 1.0 %copy.11 = f32[256,8,128]{2,1,0:T(8,128)} copy(f32[256,8,128]{2,1,0:T(8,128)S(1)} %bitcast.5) | data formatting | bytes 2097152

commit v4 on v3

--- a/solution.py
+++ b/solution.py
@@ -12,15 +12,16 @@
 BF = jnp.bfloat16
 F32 = jnp.float32
 LANES = 128
-PLANE = 1
-PLANE_AT = 6
+PLANE = 2
+PLANE_AT = 5
 GROUP = 4
 EARLY = 2
 W1 = -2
-W2 = 1
+W2 = -1
 W3 = 3
 W4 = 5
 W5 = 7
+NOTES_AT = 2
 AHEAD_END = 0
 AHEAD_MID = 2
 DIRECT = 1
@@ -168,10 +169,10 @@
             (lens_hbm, lens_ref), (home_hbm, home_ref),
         ])
     ]
-    for n in (4, 2, 3, 0):
+    loads[0].start()
+    cot_load(0).start()
+    for n in (1, 4, 2, 3):
         loads[n].start()
-    cot_load(0).start()
-    loads[1].start()
     for i in range(1, fields - 1):
         cot_load(i).start()
 
@@ -213,7 +214,6 @@
             notes[0, z, :, k, :] = note
             notes_p[0, spot, :, k, :] = note[:PLANE]
 
-    write_notes()
     loads[0].wait()
     lax.fori_loop(0, samples, spread_out, 0, unroll=8)
     loads[1].wait()
@@ -254,12 +254,6 @@
             gath[i - PLANE, 0, z] = total.astype(BF)
         if i == 0:
             pl.semaphore_wait(barrier, nz - 1 + npc - 1 + 1)
-            for d in range(1, nz):
-                m_copy(d, z).start()
-            ms_copy(z).start()
-            for d in range(1, npc):
-                n_copy(d, spot).start()
-            ns_copy(spot).start()
         if i < PLANE:
             for d in range(npc - 1, 0, -1):
                 g_copy(i, d, spot).start()
@@ -267,6 +261,14 @@
         else:
             send_own(lambda up, hop: z_copy(i, z, up, hop), i < PLANE + EARLY)
             s_copy(i, z).start()
+        if i == NOTES_AT:
+            write_notes()
+            for d in range(1, nz):
+                m_copy(d, z).start()
+            ms_copy(z).start()
+            for d in range(1, npc):
+                n_copy(d, spot).start()
+            ns_copy(spot).start()
         if i < fields - 1:
             upper_b[i] = upper
             proj_f[i] = jnp.dot(mine, bil_ref[i], preferred_element_type=F32)
@@ -595,12 +597,6 @@
     wb_copy(1 - c).wait_recv()
     wout_ref[...] = w3[...].astype(F32)
 
-    def late_last(f, carry):
-        last_step(f)
-        return carry
-
-    lax.fori_loop(max(PLANE, fields - LAG_FINAL), fields, late_last, 0)
-
     def sent(ref, sem):
         remote(ref, ref, sem, zr.at[0], sibling).wait_send()
 
@@ -617,9 +613,6 @@
         m_copy(d, z).wait_send()
     sent(notes.at[0], ms.at[1])
     sent(gath.at[:, 0], ss.at[0])
-    two_step = range(PLANE, fields - DIRECT)
-    n1 = sum(ny if f % 2 == 0 else npc - 2 for f in two_step) + DIRECT * (npc - 1)
-    n2 = sum(ny - 1 if f % 2 == 0 else 1 for f in two_step)
     if PLANE:
         for d in range(1, npc):
             n_copy(d, spot).wait_send()
@@ -628,8 +621,6 @@
         sent(notes_p.at[0], ns.at[1])
         sent(gath_p.at[:, 0], gs.at[1])
         sent(part_z, hs.at[0])
-    sent(part1.at[pl.ds(0, n1)], p1s.at[0])
-    sent(part2.at[pl.ds(0, n2)], p2s.at[0])
     wa_copy().wait_send()
     wb_copy(c).wait_send()
     for d in range(1, nz):
@@ -638,6 +629,18 @@
     for d in range(1, npc):
         w1_copy(d).wait_send()
         w3_copy(d, c * npc + spot).wait_send()
+
+    def late_last(f, carry):
+        last_step(f)
+        return carry
+
+    lax.fori_loop(max(PLANE, fields - LAG_FINAL), fields, late_last, 0)
+
+    two_step = range(PLANE, fields - DIRECT)
+    n1 = sum(ny if f % 2 == 0 else npc - 2 for f in two_step) + DIRECT * (npc - 1)
+    n2 = sum(ny - 1 if f % 2 == 0 else 1 for f in two_step)
+    sent(part1.at[pl.ds(0, n1)], p1s.at[0])
+    sent(part2.at[pl.ds(0, n2)], p2s.at[0])
 
 
 def on_device(size_gx, size_gy, pooled, cotangent, bilinear, bag_ids, bag_lens, row_home):

time: 45.2 us -> 43.4 us (0.960)
  Pallas kernels: 42.7 us -> 40.9 us
    pallas_call x1, Pallas kernels: 42.7 us -> 40.9 us  [on_device(): pl.pallas_call(functools.partial(kernel, size_gx, size_gy), out_shape=(ja...]
where the time goes in v4:
time: 43.4 us; the launch traced here: 43.2 us
  Pallas kernels  40.9 us (94%)
  local copies, waits for them, and re-layouts  1.74 us (4%)
  between operations  0.64 us (1%)
    pallas_call x1, Pallas kernels, on_device(): pl.pallas_call(functools.partial(kernel, size_gx, size_gy), out_shape=(ja...  40.9 us
    unnamed x2, local copies, waits for them, and re-layouts  1.74 us

profile of v4, /device:TPU:0, one launch (start us, length us, event | category | flops | bytes accessed | tf_op | source)
XLA Modules:
  0.0 43.2 jit_solution(7950860486071253650)
XLA Ops:
  0.6 40.9 %shard_map.77 = (f32[2048,128]{1,0:T(8,128)S(1)}, f32[8,112,128]{2,1,0:T(8,128)S(1)}) custom-call(bf16[128,8,128]{2,1,0:T(8,128)(2,1)} %pooled_hbm.1, bf16[28,128,128]{2,1,0:T(8,128)(2,1)} %bitcast.7, bf16[7,128,128]{2,1,0:T(8,128)(2,1)} %bil_hbm.1, s32[8,4,128]{2,1,0:T(4,128)} %bitcast.8, s32[8,128]{1,0:T(8,128)} %bitcast.9, s32[8,8192]{1,0:T(8,128)} %home_hbm.1), custom_call_target="tpu_custom_call" | custom-call | tf_op jit(solution)/shard_map/pallas_call | solution.py:692
  41.5 0.8 %copy.10 = f32[7,128,128]{2,1,0:T(8,128)} copy(f32[7,128,128]{2,1,0:T(8,128)S(1)} %bitcast.6) | data formatting | bytes 917504
  42.3 1.0 %copy.11 = f32[256,8,128]{2,1,0:T(8,128)} copy(f32[256,8,128]{2,1,0:T(8,128)S(1)} %bitcast.5) | data formatting | bytes 2097152

commit v5 on v4

--- a/solution.py
+++ b/solution.py
@@ -15,7 +15,7 @@
 PLANE = 2
 PLANE_AT = 5
 GROUP = 4
-EARLY = 2
+EARLY = 3
 W1 = -2
 W2 = -1
 W3 = 3
@@ -25,7 +25,7 @@
 AHEAD_END = 0
 AHEAD_MID = 2
 DIRECT = 1
-LAG_SECOND = 2
+LAG_SECOND = 3
 LAG_FINAL = 8
 
 

time: 43.4 us -> 43.2 us (level)
  no operation moved by 1% of the time
where the time goes in v5:
time: 43.2 us; the launch traced here: 43.1 us
  Pallas kernels  40.7 us (94%)
  local copies, waits for them, and re-layouts  1.74 us (4%)
  between operations  0.64 us (1%)
    pallas_call x1, Pallas kernels, on_device(): pl.pallas_call(functools.partial(kernel, size_gx, size_gy), out_shape=(ja...  40.7 us
    unnamed x2, local copies, waits for them, and re-layouts  1.74 us

profile of v5, /device:TPU:0, one launch (start us, length us, event | category | flops | bytes accessed | tf_op | source)
XLA Modules:
  0.0 43.1 jit_solution(10503258592300517570)
XLA Ops:
  0.6 40.7 %shard_map.77 = (f32[2048,128]{1,0:T(8,128)S(1)}, f32[8,112,128]{2,1,0:T(8,128)S(1)}) custom-call(bf16[128,8,128]{2,1,0:T(8,128)(2,1)} %pooled_hbm.1, bf16[28,128,128]{2,1,0:T(8,128)(2,1)} %bitcast.7, bf16[7,128,128]{2,1,0:T(8,128)(2,1)} %bil_hbm.1, s32[8,4,128]{2,1,0:T(4,128)} %bitcast.8, s32[8,128]{1,0:T(8,128)} %bitcast.9, s32[8,8192]{1,0:T(8,128)} %home_hbm.1), custom_call_target="tpu_custom_call" | custom-call | tf_op jit(solution)/shard_map/pallas_call | solution.py:692
  41.4 0.8 %copy.10 = f32[7,128,128]{2,1,0:T(8,128)} copy(f32[7,128,128]{2,1,0:T(8,128)S(1)} %bitcast.6) | data formatting | bytes 917504
  42.1 1.0 %copy.11 = f32[256,8,128]{2,1,0:T(8,128)} copy(f32[256,8,128]{2,1,0:T(8,128)S(1)} %bitcast.5) | data formatting | bytes 2097152
